TPU v7x, 32 devices: a whole 2x2x4 slice. The times are simulated.
32 devices in a mesh: wide: 8 (over z, y), narrow: 4 (over x, core).
Axes of the slice: x: 2, y: 2, z: 4, core: 2. Of those that a mesh axis runs over, the one named last changes fastest.
Arguments:
- layer_in: bfloat16 [8, 512, 1536], P('wide', 'narrow'), may hold values from -6 to 6
- lengths: int32 [8, 8], P('wide'), may hold values from 1 to 256, 512 in all within a row
- w_qkv: bfloat16 [1536, 2048], P(('wide', 'narrow')), may hold values from -0.15625 to 0.15625
- b_qkv: bfloat16 [2048], P(('wide', 'narrow')), may hold values from -3 to 3
- w_out: bfloat16 [1536, 1536], P(None, ('wide', 'narrow')), may hold values from -0.625 to 0.625
- norm1_gain: bfloat16 [1536], P(('wide', 'narrow')), may hold values from 0.099609375 to 1.8984375
- norm2_gain: bfloat16 [1536], P(('wide', 'narrow')), may hold values from 0.099609375 to 1.8984375
- w_gate: bfloat16 [1536, 8960], P('wide', 'narrow'), may hold values from -0.15625 to 0.15625
- w_up: bfloat16 [1536, 8960], P('wide', 'narrow'), may hold values from -0.15625 to 0.15625
- w_down: bfloat16 [8960, 1536], P('narrow', 'wide'), may hold values from -0.0625 to 0.0625
- grad_out: bfloat16 [8, 512, 1536], P('wide', 'narrow'), may hold values from -6 to 6
Outputs:
- layer_out: bfloat16 [8, 512, 1536], P('wide', 'narrow')
- grad_in: float32 [8, 512, 1536], P('wide', 'narrow')
- grad_w_qkv: float32 [1536, 2048], P(('wide', 'narrow'))
- grad_b_qkv: float32 [2048], P(('wide', 'narrow'))
- grad_w_out: float32 [1536, 1536], P(None, ('wide', 'narrow'))
- grad_norm1: float32 [1536], P(('wide', 'narrow'))
- grad_norm2: float32 [1536], P(('wide', 'narrow'))
- grad_w_gate: float32 [1536, 8960], P('wide', 'narrow')
- grad_w_up: float32 [1536, 8960], P('wide', 'narrow')
- grad_w_down: float32 [8960, 1536], P('narrow', 'wide')
Inputs may be any that keep to these rules, and one draw needn't show every extreme that they name: In each pack the 8 lengths sum to 512, and one of them is 256.
All inputs are finite; a program needn't handle non-finite values.
Results may differ from a plain program's by a relative error of at most 0.02.
Values may be sent and summed in bfloat16 or wider, within the bound.
A program may use at most 192 MiB of HBM per device.

v0:
```python
import math
import jax
import jax.numpy as jnp
from jax import lax
from jax.sharding import PartitionSpec as P

QUERY_HEADS = 12
KEY_VALUE_HEADS = 2
HEAD_WIDTH = 128
EPSILON = 1e-06
ROPE_BASE = 10000.0
NEGATIVE_BIG = -1e30
HIGHEST = lax.Precision.HIGHEST


def rms_scale(value_rows, gain):
    return (
        value_rows
        * lax.rsqrt(jnp.mean(value_rows * value_rows, axis=-1, keepdims=True) + EPSILON)
        * gain
    )


def apply_rotation(value_rows, token_position):
    half_dim = value_rows.shape[-1] // 2
    freq = jnp.exp(
        jnp.arange(half_dim, dtype=jnp.float32)
        * (-2.0 * math.log(ROPE_BASE) / value_rows.shape[-1])
    )
    angle = token_position[:, None] * freq[None, :]
    cosine = jnp.cos(angle)[:, None, :]
    sine = jnp.sin(angle)[:, None, :]
    leading = value_rows[..., :half_dim]
    trailing = value_rows[..., half_dim:]
    return jnp.concatenate(
        [leading * cosine - trailing * sine, trailing * cosine + leading * sine], axis=-1
    )


def doc_layout(index, doc_lengths):
    ends = jnp.cumsum(doc_lengths)
    starts = ends - doc_lengths
    document_index = jnp.sum((index[:, None] >= ends[None, :]).astype(jnp.int32), axis=1)
    onehot = (
        document_index[:, None] == jnp.arange(doc_lengths.shape[0], dtype=jnp.int32)[None, :]
    ).astype(jnp.int32)
    token_position = index - jnp.sum(onehot * starts[None, :], axis=1)
    return (document_index, token_position.astype(jnp.float32))


def contract_rows(left, right):
    return lax.dot_general(
        left, right, (((0,), (0,)), ((), ())), preferred_element_type=jnp.float32
    )


def times_transposed(left, right):
    return lax.dot_general(
        left, right, (((1,), (1,)), ((), ())), preferred_element_type=jnp.float32
    )


def shards(
    layer_in, lengths, w_qkv, b_qkv, w_out, norm1_gain, norm2_gain, w_gate, w_up, w_down, grad_out
):
    hidden_in = layer_in[0].astype(jnp.float32)
    rows_per_shard = hidden_in.shape[0]
    narrow_count = lax.axis_size("narrow")
    first_row = lax.axis_index("narrow") * rows_per_shard
    pack_rows = rows_per_shard * narrow_count
    query_group = QUERY_HEADS // KEY_VALUE_HEADS
    query_total_width = QUERY_HEADS * HEAD_WIDTH
    key_total_width = KEY_VALUE_HEADS * HEAD_WIDTH
    scale = HEAD_WIDTH ** (-0.5)
    doc_lengths = lengths[0]
    local_index = first_row + jnp.arange(rows_per_shard, dtype=jnp.int32)
    local_doc, local_pos = doc_layout(local_index, doc_lengths)
    key_index = jnp.arange(pack_rows, dtype=jnp.int32)
    key_doc = doc_layout(key_index, doc_lengths)[0]
    wqkv_full, bias_full, wout_full, gain_one, gain_two = (
        lax.all_gather(w_qkv, ("wide", "narrow"), axis=0, tiled=True),
        lax.all_gather(b_qkv, ("wide", "narrow"), axis=0, tiled=True),
        lax.all_gather(w_out, ("wide", "narrow"), axis=1, tiled=True),
        lax.all_gather(norm1_gain, ("wide", "narrow"), axis=0, tiled=True),
        lax.all_gather(norm2_gain, ("wide", "narrow"), axis=0, tiled=True),
    )
    wgate_full, wup_full, wdown_full = (
        lax.all_gather(w_gate, "wide", axis=0, tiled=True),
        lax.all_gather(w_up, "wide", axis=0, tiled=True),
        lax.all_gather(w_down, "wide", axis=1, tiled=True),
    )
    gain_one = gain_one.astype(jnp.float32)
    gain_two = gain_two.astype(jnp.float32)
    normed_one = rms_scale(hidden_in, gain_one).astype(jnp.bfloat16)
    unrotated_projection = jnp.dot(
        normed_one, wqkv_full, preferred_element_type=jnp.float32
    ) + bias_full.astype(jnp.float32)
    pre_query = unrotated_projection[:, :query_total_width].reshape(
        rows_per_shard, QUERY_HEADS, HEAD_WIDTH
    )
    unrotated_key = unrotated_projection[
        :, query_total_width : query_total_width + key_total_width
    ].reshape(rows_per_shard, KEY_VALUE_HEADS, HEAD_WIDTH)

    def rotate_local(value_rows):
        return apply_rotation(value_rows, local_pos)

    rotated_query, query_back = jax.vjp(rotate_local, pre_query)
    key_rot, key_backward = jax.vjp(rotate_local, unrotated_key)
    query_rows = rotated_query.astype(jnp.bfloat16).reshape(
        rows_per_shard, KEY_VALUE_HEADS, query_group, HEAD_WIDTH
    )
    key_local = key_rot.reshape(rows_per_shard, key_total_width).astype(jnp.bfloat16)
    value_local = unrotated_projection[:, query_total_width + key_total_width :].astype(
        jnp.bfloat16
    )
    every_key_row, every_value_row = (
        lax.all_gather(key_local, "narrow", axis=0, tiled=True),
        lax.all_gather(value_local, "narrow", axis=0, tiled=True),
    )
    rows_per_block = min(512, pack_rows)
    count_of_blocks = pack_rows // rows_per_block
    blocked_keys = every_key_row.reshape(
        count_of_blocks, rows_per_block, KEY_VALUE_HEADS, HEAD_WIDTH
    )
    blocked_values = every_value_row.reshape(
        count_of_blocks, rows_per_block, KEY_VALUE_HEADS, HEAD_WIDTH
    )
    doc_blocks = key_doc.reshape(count_of_blocks, rows_per_block)
    index_blocks = key_index.reshape(count_of_blocks, rows_per_block)
    input_per_block = (blocked_keys, blocked_values, doc_blocks, index_blocks)

    def block_scores(key_block, doc_block, index_block):
        scores = (
            jnp.einsum("tkgd,skd->kgts", query_rows, key_block, preferred_element_type=jnp.float32)
            * scale
        )
        allowed = (local_doc[:, None] == doc_block[None, :]) & (
            index_block[None, :] <= local_index[:, None]
        )
        return (jnp.where(allowed, scores, NEGATIVE_BIG), allowed)

    def total_block(carry, inputs):
        running_max, running_sum = carry
        key_block, value_block, doc_block, index_block = inputs
        masked, allowed = block_scores(key_block, doc_block, index_block)
        new_max = jnp.maximum(running_max, jnp.max(masked, axis=-1))
        probs = jnp.where(allowed, jnp.exp(masked - new_max[..., None]), 0.0)
        running_sum = running_sum * jnp.exp(running_max - new_max) + jnp.sum(probs, axis=-1)
        return ((new_max, running_sum), None)

    start_carry = (
        jnp.full((KEY_VALUE_HEADS, query_group, rows_per_shard), NEGATIVE_BIG, jnp.float32),
        jnp.zeros((KEY_VALUE_HEADS, query_group, rows_per_shard), jnp.float32),
    )
    (final_max, final_sum), _ = lax.scan(total_block, start_carry, input_per_block)
    log_total = final_max + jnp.log(final_sum)

    def block_probs(key_block, doc_block, index_block):
        masked, allowed = block_scores(key_block, doc_block, index_block)
        return jnp.where(allowed, jnp.exp(masked - log_total[..., None]), 0.0)

    def block_forward_pass(weighted, inputs):
        key_block, value_block, doc_block, index_block = inputs
        probs_low = block_probs(key_block, doc_block, index_block).astype(jnp.bfloat16)
        weighted = weighted + jnp.einsum(
            "kgts,skd->kgtd", probs_low, value_block, preferred_element_type=jnp.float32
        )
        return (weighted, None)

    attn_heads, _ = lax.scan(
        block_forward_pass,
        jnp.zeros((KEY_VALUE_HEADS, query_group, rows_per_shard, HEAD_WIDTH), jnp.float32),
        input_per_block,
    )
    attn_low = (
        attn_heads.transpose(2, 0, 1, 3)
        .reshape(rows_per_shard, query_total_width)
        .astype(jnp.bfloat16)
    )
    middle = hidden_in + jnp.dot(attn_low, wout_full, preferred_element_type=jnp.float32)
    normed_two = rms_scale(middle, gain_two).astype(jnp.bfloat16)
    pack_normed = lax.all_gather(normed_two, "narrow", axis=0, tiled=True)
    gate = jnp.dot(pack_normed, wgate_full, preferred_element_type=jnp.float32)
    up_part = jnp.dot(pack_normed, wup_full, preferred_element_type=jnp.float32)
    sigmoid_gate = jax.nn.sigmoid(gate)
    activated = gate * sigmoid_gate
    hidden_act = (activated * up_part).astype(jnp.bfloat16)
    mixed = lax.psum_scatter(
        jnp.dot(hidden_act, wdown_full, preferred_element_type=jnp.float32).astype(jnp.bfloat16),
        "narrow",
        scatter_dimension=0,
        tiled=True,
    ).astype(jnp.float32)
    layer_out = (middle + mixed).astype(jnp.bfloat16)
    wgate_back, wup_back, wdown_back = (
        lax.all_gather(w_gate, "wide", axis=0, tiled=True),
        lax.all_gather(w_up, "wide", axis=0, tiled=True),
        lax.all_gather(w_down, "wide", axis=1, tiled=True),
    )
    cotangent = grad_out[0]
    pack_cotangent = lax.all_gather(cotangent, "narrow", axis=0, tiled=True)
    grad_hidden = times_transposed(pack_cotangent, wdown_back)
    grad_wdown = contract_rows(hidden_act, pack_cotangent)
    grad_gate = (grad_hidden * up_part * sigmoid_gate * (1.0 + gate * (1.0 - sigmoid_gate))).astype(
        jnp.bfloat16
    )
    grad_up = (grad_hidden * activated).astype(jnp.bfloat16)
    grad_wgate = contract_rows(pack_normed, grad_gate)
    grad_wup = contract_rows(pack_normed, grad_up)
    grad_normed_two = lax.psum_scatter(
        (times_transposed(grad_gate, wgate_back) + times_transposed(grad_up, wup_back)).astype(
            jnp.bfloat16
        ),
        "narrow",
        scatter_dimension=0,
        tiled=True,
    ).astype(jnp.float32)
    norm_two_back = jax.vjp(rms_scale, middle, gain_two)[1]
    grad_middle_norm, grad_gain_two = norm_two_back(grad_normed_two)
    grad_middle = cotangent.astype(jnp.float32) + grad_middle_norm
    grad_attn_proj = grad_middle.astype(jnp.bfloat16)
    grad_wout = contract_rows(attn_low, grad_attn_proj)
    attention_gradient = times_transposed(grad_attn_proj, wout_full).astype(jnp.bfloat16)
    head_gradients = attention_gradient.reshape(
        rows_per_shard, KEY_VALUE_HEADS, query_group, HEAD_WIDTH
    )
    delta = jnp.einsum(
        "tkgd,kgtd->kgt", head_gradients.astype(jnp.float32), attn_heads, precision=HIGHEST
    )

    def block_backward_pass(grad_query, inputs):
        key_block, value_block, doc_block, index_block = inputs
        probs = block_probs(key_block, doc_block, index_block)
        grad_probs = jnp.einsum(
            "tkgd,skd->kgts", head_gradients, value_block, preferred_element_type=jnp.float32
        )
        grad_scores = (probs * (grad_probs - delta[..., None])).astype(jnp.bfloat16)
        grad_query = (
            grad_query
            + jnp.einsum(
                "kgts,skd->tkgd", grad_scores, key_block, preferred_element_type=jnp.float32
            )
            * scale
        )
        grad_key = (
            jnp.einsum(
                "kgts,tkgd->skd", grad_scores, query_rows, preferred_element_type=jnp.float32
            )
            * scale
        )
        grad_value = jnp.einsum(
            "kgts,tkgd->skd",
            probs.astype(jnp.bfloat16),
            head_gradients,
            preferred_element_type=jnp.float32,
        )
        return (grad_query, (grad_key, grad_value))

    grad_query, (grad_key_blocks, grad_value_blocks) = lax.scan(
        block_backward_pass,
        jnp.zeros((rows_per_shard, KEY_VALUE_HEADS, query_group, HEAD_WIDTH), jnp.float32),
        input_per_block,
    )
    local_key_gradients, grad_values_local = (
        lax.psum_scatter(
            grad_key_blocks.reshape(pack_rows, key_total_width).astype(jnp.bfloat16),
            "narrow",
            scatter_dimension=0,
            tiled=True,
        ).astype(jnp.float32),
        lax.psum_scatter(
            grad_value_blocks.reshape(pack_rows, key_total_width).astype(jnp.bfloat16),
            "narrow",
            scatter_dimension=0,
            tiled=True,
        ).astype(jnp.float32),
    )
    grad_pre_query = query_back(grad_query.reshape(rows_per_shard, QUERY_HEADS, HEAD_WIDTH))[0]
    unrotated_key_gradient = key_backward(
        local_key_gradients.reshape(rows_per_shard, KEY_VALUE_HEADS, HEAD_WIDTH)
    )[0]
    grad_pre = jnp.concatenate(
        [
            grad_pre_query.reshape(rows_per_shard, query_total_width),
            unrotated_key_gradient.reshape(rows_per_shard, key_total_width),
            grad_values_local,
        ],
        axis=1,
    ).astype(jnp.bfloat16)
    grad_bias = jnp.sum(grad_pre.astype(jnp.float32), axis=0)
    grad_wqkv = contract_rows(normed_one, grad_pre)
    grad_normed_one = times_transposed(grad_pre, wqkv_full)
    norm_one_back = jax.vjp(rms_scale, hidden_in, gain_one)[1]
    grad_input_norm, grad_gain_one = norm_one_back(grad_normed_one)
    grad_input = grad_middle + grad_input_norm
    sum_wqkv, sum_bias, sum_wout, sum_gain_one, sum_gain_two = (
        lax.psum_scatter(grad_wqkv, ("wide", "narrow"), scatter_dimension=0, tiled=True),
        lax.psum_scatter(grad_bias, ("wide", "narrow"), scatter_dimension=0, tiled=True),
        lax.psum_scatter(grad_wout, ("wide", "narrow"), scatter_dimension=1, tiled=True),
        lax.psum_scatter(grad_gain_one, ("wide", "narrow"), scatter_dimension=0, tiled=True),
        lax.psum_scatter(grad_gain_two, ("wide", "narrow"), scatter_dimension=0, tiled=True),
    )
    sum_wgate, sum_wup, sum_wdown = (
        lax.psum_scatter(
            grad_wgate.astype(jnp.bfloat16), "wide", scatter_dimension=0, tiled=True
        ).astype(jnp.float32),
        lax.psum_scatter(
            grad_wup.astype(jnp.bfloat16), "wide", scatter_dimension=0, tiled=True
        ).astype(jnp.float32),
        lax.psum_scatter(
            grad_wdown.astype(jnp.bfloat16), "wide", scatter_dimension=1, tiled=True
        ).astype(jnp.float32),
    )
    return (
        layer_out[None],
        grad_input[None],
        sum_wqkv,
        sum_bias,
        sum_wout,
        sum_gain_one,
        sum_gain_two,
        sum_wgate,
        sum_wup,
        sum_wdown,
    )


def solution(mesh):
    placed = (
        P("wide", "narrow", None),
        P("wide", None),
        P(("wide", "narrow"), None),
        P(("wide", "narrow")),
        P(None, ("wide", "narrow")),
        P(("wide", "narrow")),
        P(("wide", "narrow")),
        P("wide", "narrow"),
        P("wide", "narrow"),
        P("narrow", "wide"),
        P("wide", "narrow", None),
    )
    return jax.shard_map(
        shards,
        mesh=mesh,
        in_specs=placed,
        out_specs=(
            P("wide", "narrow", None),
            P("wide", "narrow", None),
            P(("wide", "narrow"), None),
            P(("wide", "narrow")),
            P(None, ("wide", "narrow")),
            P(("wide", "narrow")),
            P(("wide", "narrow")),
            P("wide", "narrow"),
            P("wide", "narrow"),
            P("narrow", "wide"),
        ),
        check_vma=False,
    )
```

profile of v0, /device:TPU:0, one launch (start us, length us, event | category | flops | bytes accessed | tf_op | source)
XLA Modules:
  0.0 1367.8 jit_solution(4092313823965801265)
XLA Ops:
  12.0 42.5 %all-reduce.11 = (bf16[2048]{0:T(1024)(128)(2,1)S(1)}, bf16[1536]{0:T(1024)(128)(2,1)S(1)}, bf16[1536]{0:T(1024)(128)(2,1)S(1)}) all-reduce(bf16[2048]{0:T(1024)(128)(2,1)S(1)} %dynamic-update-slice.1, bf16[1536]{0:T(1024)(128)(2,1)S(1)} %dynamic-update-slice, ...), channel_id=1, replica_groups=mesh['wide'=8,'narrow'=4] {'wide','narrow'}, use_global_device_ids=true, to_apply=%add.5 | all-reduce | flops 5120 | bytes 20480
  58.7 24.4 %all-gather.9.cloned.1.call-done = bf16[1536,2048]{1,0:T(8,128)(2,1)} async-done(((bf16[48,2048]{1,0:T(8,128)(2,1)}), bf16[1536,2048]{1,0:T(8,128)(2,1)}) %all-gather.9.cloned.1.call-update) | async-done | bytes 6291472 | tf_op jit(solution)/shard_map/all_gather | solution.py:81
  83.1 4.0 convolution_add_fusion.2
  89.4 5.8 all_gather.43
  96.1 5.9 all_gather.42
  108.1 40.1 %all-gather.11.cloned.1.call-done = bf16[1536,1536]{0,1:T(8,128)(2,1)} async-done(((bf16[1536,48]{0,1:T(8,128)(2,1)}), bf16[1536,1536]{0,1:T(8,128)(2,1)}) %all-gather.11.cloned.1.call-update) | async-done | bytes 4718608 | tf_op jit(solution)/shard_map/all_gather | solution.py:83
  148.2 4.2 multiply_reduce_fusion
  156.5 100.5 %all-gather.15.cloned.1.call-done = bf16[1536,2240]{1,0:T(8,128)(2,1)} async-done(((bf16[192,2240]{1,0:T(8,128)(2,1)}), bf16[1536,2240]{1,0:T(8,128)(2,1)}) %all-gather.15.cloned.1.call-update) | async-done | bytes 6881296 | tf_op jit(solution)/shard_map/all_gather | solution.py:88
  257.0 19.8 %all-gather.13.cloned.1.call-done = bf16[512,1536]{1,0:T(8,128)(2,1)} async-done(((bf16[128,1536]{1,0:T(8,128)(2,1)}), bf16[512,1536]{1,0:T(8,128)(2,1)}) %all-gather.13.cloned.1.call-update) | async-done | bytes 1572880 | tf_op jit(solution)/shard_map/all_gather | solution.py:183
  276.8 9.5 fusion.47
  286.3 100.9 %all-gather.17.cloned.1.call-done = bf16[1536,2240]{1,0:T(8,128)(2,1)} async-done(((bf16[192,2240]{1,0:T(8,128)(2,1)}), bf16[1536,2240]{1,0:T(8,128)(2,1)}) %all-gather.17.cloned.1.call-update) | async-done | bytes 6881296 | tf_op jit(solution)/shard_map/all_gather | solution.py:89
  387.2 9.3 fusion.48
  396.5 9.9 all-gather.21.cloned.1.call-done
  406.5 110.5 %all-gather.19.cloned.1.call-done = bf16[2240,1536]{0,1:T(8,128)(2,1)} async-done(((bf16[2240,192]{0,1:T(8,128)(2,1)}), bf16[2240,1536]{0,1:T(8,128)(2,1)}) %all-gather.19.cloned.1.call-update) | async-done | bytes 6881296 | tf_op jit(solution)/shard_map/all_gather | solution.py:90
  517.0 13.3 multiply_convert_fusion
  530.3 7.8 fusion.49
  538.2 5.0 fusion.3
  543.3 8.8 convolution_convert_fusion.3
  552.5 17.1 %reduce-scatter.16.cloned.1.call-done = bf16[128,1536]{1,0:T(8,128)(2,1)} async-done(((bf16[512,1536]{1,0:T(8,128)(2,1)}), bf16[128,1536]{1,0:T(8,128)(2,1)}) %reduce-scatter.16.cloned.1.call-update) | async-done | bytes 393232 | tf_op jit(solution)/shard_map/reduce_scatter | solution.py:211
  572.8 27.9 %reduce-scatter.14.cloned.1.call-done = bf16[128,1536]{1,0:T(8,128)(2,1)} async-done(((bf16[512,1536]{1,0:T(8,128)(2,1)}), bf16[128,1536]{1,0:T(8,128)(2,1)}) %reduce-scatter.14.cloned.1.call-update) | async-done | bytes 393232 | tf_op jit(solution)/shard_map/reduce_scatter | solution.py:189
  622.7 8.9 convolution_convert_fusion.2
  633.1 7.6 convolution_convert_fusion.1
  642.1 7.5 convolution_convert_fusion
  650.8 5.0 fusion.28
  662.5 6.4 fusion.31
  669.2 5.1 fusion.17
  674.3 43.1 %all-reduce.10 = (f32[2048]{0:T(1024)S(1)}, f32[1536]{0:T(1024)S(1)}, f32[1536]{0:T(1024)S(1)}) all-reduce(f32[2048]{0:T(1024)S(1)} %convert_reduce_fusion, f32[1536]{0:T(1024)S(1)} %get-tuple-element.83, f32[1536]{0:T(1024)S(1)} %copy-done.22), channel_id=8, replica_groups=mesh['wide'=8,'narrow'=4] {'wide','narrow'}, use_global_device_ids=true, to_apply=%region_16.17.clone | all-reduce | flops 5120 | bytes 40960
  720.3 75.0 %reduce-scatter.22.cloned.1.call-done = bf16[192,2240]{1,0:T(8,128)(2,1)} async-done(((bf16[1536,2240]{1,0:T(8,128)(2,1)}), bf16[192,2240]{1,0:T(8,128)(2,1)}) %reduce-scatter.22.cloned.1.call-update) | async-done | bytes 860176 | tf_op jit(solution)/shard_map/reduce_scatter | solution.py:305
  797.8 129.5 %reduce-scatter.24.cloned.1.call-done = bf16[192,2240]{1,0:T(8,128)(2,1)} async-done(((bf16[1536,2240]{1,0:T(8,128)(2,1)}), bf16[192,2240]{1,0:T(8,128)(2,1)}) %reduce-scatter.24.cloned.1.call-update) | async-done | bytes 860176 | tf_op jit(solution)/shard_map/reduce_scatter | solution.py:308
  929.8 129.4 %reduce-scatter.26.cloned.1.call-done = bf16[2240,192]{0,1:T(8,128)(2,1)} async-done(((bf16[2240,1536]{0,1:T(8,128)(2,1)}), bf16[2240,192]{0,1:T(8,128)(2,1)}) %reduce-scatter.26.cloned.1.call-update) | async-done | bytes 860176 | tf_op jit(solution)/shard_map/reduce_scatter | solution.py:311
  1061.6 139.1 %reduce-scatter.20.cloned.1.call-done = f32[1536,48]{0,1:T(8,128)} async-done(((f32[1536,1536]{0,1:T(8,128)}), f32[1536,48]{0,1:T(8,128)}) %reduce-scatter.20.cloned.1.call-update) | async-done | bytes 294928 | tf_op jit(solution)/shard_map/reduce_scatter | solution.py:300
  1200.8 160.3 %reduce-scatter.18.cloned.1.call-done = f32[48,2048]{1,0:T(8,128)} async-done(((f32[1536,2048]{1,0:T(8,128)}), f32[48,2048]{1,0:T(8,128)}) %reduce-scatter.18.cloned.1.call-update) | async-done | bytes 393232 | tf_op jit(solution)/shard_map/reduce_scatter | solution.py:298
  (183 shorter events, 68.8 us)
Async XLA Ops:
  7.2 75.9 %all-gather.9.cloned.1.call-start = ((), (), s32[]{:S(2)}) async-start(), calls=%async_computation.9 | async-start | bytes 6488064 | tf_op jit(solution)/shard_map/all_gather | solution.py:81
  7.9 140.3 %all-gather.11.cloned.1.call-start = ((), (), s32[]{:S(2)}) async-start(), calls=%async_computation.10 | async-start | bytes 4866048 | tf_op jit(solution)/shard_map/all_gather | solution.py:83
  8.7 248.4 %all-gather.15.cloned.1.call-start = ((), (), s32[]{:S(2)}) async-start(), calls=%async_computation.12 | async-start | bytes 7962624 | tf_op jit(solution)/shard_map/all_gather | solution.py:88
  9.4 267.4 %all-gather.13.cloned.1.call-start = ((), (), s32[]{:S(2)}) async-start(), calls=%async_computation.11 | async-start | bytes 1966080 | tf_op jit(solution)/shard_map/all_gather | solution.py:183
  56.5 31.0 %copy-start.12 = (f32[128,64]{1,0:T(8,128)}, f32[128,64]{1,0:T(8,128)S(1)}, u32[]{:S(2)}) copy-start(f32[128,64]{1,0:T(8,128)S(1)} %get-tuple-element.136) | copy-start | bytes 98308
  56.5 31.0 %copy-start.14 = (f32[128,64]{1,0:T(8,128)}, f32[128,64]{1,0:T(8,128)S(1)}, u32[]{:S(2)}) copy-start(f32[128,64]{1,0:T(8,128)S(1)} %get-tuple-element.137) | copy-start | bytes 98308
  56.6 31.5 %copy-start.17 = (f32[128,64]{0,1:T(8,128)}, f32[128,64]{0,1:T(8,128)S(1)}, u32[]{:S(2)}) copy-start(f32[128,64]{0,1:T(8,128)S(1)} %copy.113) | copy-start | bytes 98308
  56.7 31.4 %copy-start.19 = (f32[128,64]{0,1:T(8,128)}, f32[128,64]{0,1:T(8,128)S(1)}, u32[]{:S(2)}) copy-start(f32[128,64]{0,1:T(8,128)S(1)} %copy.114) | copy-start | bytes 98308
  57.9 25.2 %copy-start.28 = (f32[128]{0:T(128)}, f32[128]{0:T(128)S(1)}, u32[]{:S(2)}) copy-start(f32[128]{0:T(128)S(1)} %fusion.23) | copy-start | bytes 1540
  58.0 25.1 %copy-start.23 = (f32[128]{0:T(128)}, f32[128]{0:T(128)S(1)}, u32[]{:S(2)}) copy-start(f32[128]{0:T(128)S(1)} %fusion.36) | copy-start | bytes 1540
  88.4 15.5 %copy-start.6 = (bf16[128,12,64]{2,0,1:T(8,128)(2,1)}, bf16[128,12,64]{2,0,1:T(8,128)(2,1)S(1)}, u32[]{:S(2)}) copy-start(bf16[128,12,64]{2,0,1:T(8,128)(2,1)S(1)} %copy.115) | copy-start | bytes 589828
  102.0 4.2 copy-start.21
  105.5 42.6 %copy-start.3 = (bf16[1,128,1536]{2,1,0:T(8,128)(2,1)S(1)}, bf16[1,128,1536]{2,1,0:T(8,128)(2,1)}, u32[]{:S(2)}) copy-start(bf16[1,128,1536]{2,1,0:T(8,128)(2,1)} %param.11) | copy-start | bytes 1179652
  154.3 232.9 %all-gather.17.cloned.1.call-start = ((), (), s32[]{:S(2)}) async-start(), calls=%async_computation.13 | async-start | bytes 7962624 | tf_op jit(solution)/shard_map/all_gather | solution.py:89
  154.9 251.5 %all-gather.21.cloned.1.call-start = ((), (), s32[]{:S(2)}) async-start(), calls=%async_computation.22 | async-start | bytes 1966080 | tf_op jit(solution)/shard_map/all_gather | solution.py:202
  155.5 361.5 %all-gather.19.cloned.1.call-start = ((), (), s32[]{:S(2)}) async-start(), calls=%async_computation.14 | async-start | bytes 7962624 | tf_op jit(solution)/shard_map/all_gather | solution.py:90
  156.3 413.3 %reduce-scatter.16.cloned.1.call-start = ((), (), s32[]{:S(2)}) async-start(), calls=%async_computation.16 | async-start | bytes 1966080 | tf_op jit(solution)/shard_map/reduce_scatter | solution.py:211
  530.3 7.8 copy-start.35
  530.3 7.9 copy-start.34
  530.3 7.9 copy-start.31
  543.2 57.6 %reduce-scatter.14.cloned.1.call-start = ((), (), s32[]{:S(2)}) async-start(), calls=%async_computation.15 | async-start | bytes 1966080 | tf_op jit(solution)/shard_map/reduce_scatter | solution.py:189
  552.0 105.9 %reduce-scatter.28.cloned.1.call-start = ((), (), s32[]{:S(2)}) async-start(), calls=%async_computation.23 | async-start | bytes 327680
  604.2 7.1 copy-start.26
  618.2 43.4 %reduce-scatter.30.cloned.1.call-start = ((), (), s32[]{:S(2)}) async-start(), calls=%async_computation.24 | async-start | bytes 327680
  622.7 172.6 %reduce-scatter.22.cloned.1.call-start = ((), (), s32[]{:S(2)}) async-start(), calls=%async_computation.19 | async-start | bytes 7962624 | tf_op jit(solution)/shard_map/reduce_scatter | solution.py:305
  631.7 295.6 %reduce-scatter.24.cloned.1.call-start = ((), (), s32[]{:S(2)}) async-start(), calls=%async_computation.20 | async-start | bytes 7962624 | tf_op jit(solution)/shard_map/reduce_scatter | solution.py:308
  640.7 418.5 %reduce-scatter.26.cloned.1.call-start = ((), (), s32[]{:S(2)}) async-start(), calls=%async_computation.21 | async-start | bytes 7962624 | tf_op jit(solution)/shard_map/reduce_scatter | solution.py:311
  649.6 551.1 %reduce-scatter.20.cloned.1.call-start = ((), (), s32[]{:S(2)}) async-start(), calls=%async_computation.18 | async-start | bytes 9732096 | tf_op jit(solution)/shard_map/reduce_scatter | solution.py:300
  655.9 6.6 copy-start.24
  655.9 705.1 %reduce-scatter.18.cloned.1.call-start = ((), (), s32[]{:S(2)}) async-start(), calls=%async_computation.17 | async-start | bytes 12976128 | tf_op jit(solution)/shard_map/reduce_scatter | solution.py:298
  669.2 5.1 copy-start.22
  669.2 50.0 %copy-start.29 = (f32[128]{0:T(128)S(1)}, f32[128]{0:T(128)}, u32[]{:S(2)}) copy-start(f32[128]{0:T(128)} %copy-done.28) | copy-start | bytes 1540
  (20 other events, 35.9 us)
Sparse Core Ops, SparseCore 0:
  10.8 72.2 all-gather.8
  86.0 62.1 all-gather.10
  150.4 106.5 all-gather.14
  259.0 17.7 all-gather.12
  278.9 108.2 all-gather.16
  388.6 17.7 all-gather.20
  408.6 108.2 all-gather.18
  543.3 26.2 reduce-scatter.15
  572.7 28.0 reduce-scatter.13
  618.3 20.0 reduce-scatter.27
  641.4 20.0 reduce-scatter.29
  665.1 130.1 reduce-scatter.21
  799.0 128.2 reduce-scatter.23
  930.8 128.2 reduce-scatter.25
  1065.4 135.2 reduce-scatter.19
  1207.2 153.7 reduce-scatter.17
where the time goes:
time: 1380 us; the launch traced here: 1370 us
  waiting for transfers between devices  1090 us (79%)
  matrix products  117 us (8%)
  blocking collectives  97.3 us (7%)
  local copies, waits for them, and re-layouts  23.7 us (2%)
  other arithmetic  23 us (2%)
  between operations  14.7 us (1%)
    reduce_scatter x1, waiting for transfers between devices, shards(): lax.psum_scatter(grad_wqkv, ('wide', 'narrow'), scatter_dimension=0, tile...  160 us
    reduce_scatter x1, waiting for transfers between devices, shards(): lax.psum_scatter(grad_wout, ('wide', 'narrow'), scatter_dimension=1, tile...  139 us
    reduce_scatter x1, waiting for transfers between devices, shards(): lax.psum_scatter(grad_wup.astype(jnp.bfloat16), 'wide', scatter_dimension...  130 us
    reduce_scatter x1, waiting for transfers between devices, shards(): lax.psum_scatter(grad_wdown.astype(jnp.bfloat16), 'wide', scatter_dimensi...  129 us
    all_gather x1, waiting for transfers between devices, shards(): lax.all_gather(w_down, 'wide', axis=1, tiled=True)  111 us
    all_gather x1, waiting for transfers between devices, shards(): lax.all_gather(w_up, 'wide', axis=0, tiled=True)  101 us
    all_gather x1, waiting for transfers between devices, shards(): lax.all_gather(w_gate, 'wide', axis=0, tiled=True)  101 us
    unnamed x2, blocking collectives  85.6 us
  transfers between devices with their start and end apart: 16, of which 15 were waited for; matrix products, arithmetic and copies ran while one was open for 8% of the time, Pallas kernels for 0%

commit v1 on v0

--- a/solution.py
+++ b/solution.py
@@ -77,10 +77,19 @@
     local_doc, local_pos = doc_layout(local_index, doc_lengths)
     key_index = jnp.arange(pack_rows, dtype=jnp.int32)
     key_doc = doc_layout(key_index, doc_lengths)[0]
+    move_the_quotas = lambda base_x: jnp.concatenate(
+        lax.all_to_all(
+            jnp.stack([base_x for _ in range(lax.axis_size(("wide", "narrow")))]),
+            ("wide", "narrow"),
+            0,
+            0,
+        ),
+        axis=1,
+    )
     wqkv_full, bias_full, wout_full, gain_one, gain_two = (
         lax.all_gather(w_qkv, ("wide", "narrow"), axis=0, tiled=True),
         lax.all_gather(b_qkv, ("wide", "narrow"), axis=0, tiled=True),
-        lax.all_gather(w_out, ("wide", "narrow"), axis=1, tiled=True),
+        move_the_quotas(w_out),
         lax.all_gather(norm1_gain, ("wide", "narrow"), axis=0, tiled=True),
         lax.all_gather(norm2_gain, ("wide", "narrow"), axis=0, tiled=True),
     )

time: 1380 us -> 1370 us (level)
  waiting for transfers between devices: 1090 us -> 941 us
  blocking collectives: 97.3 us -> 233 us
    unnamed x2, blocking collectives: 85.6 us -> 221 us
    all_gather x1, waiting for transfers between devices: 101 us -> 15.7 us  [shards(): lax.all_gather(w_gate, 'wide', axis=0, tiled=True)]
    all_gather x1 -> x0, waiting for transfers between devices: 40.1 us -> none  [shards(): lax.all_gather(w_out, ('wide', 'narrow'), axis=1, tiled=True)]
    all_gather x1, waiting for transfers between devices: 24.4 us -> 0.01 us  [shards(): lax.all_gather(w_qkv, ('wide', 'narrow'), axis=0, tiled=True)]
  transfers between devices with their start and end apart: 16 -> 16, of which waited for: 15 -> 13; matrix products, arithmetic and copies ran while one was open for 8% -> 8% of each run, Pallas kernels for 0% -> 0%
where the time goes in v1:
time: 1370 us; the launch traced here: 1360 us
  waiting for transfers between devices  941 us (69%)
  blocking collectives  233 us (17%)
  matrix products  117 us (9%)
  local copies, waits for them, and re-layouts  27 us (2%)
  other arithmetic  20.7 us (2%)
  between operations  14.7 us (1%)
    unnamed x2, blocking collectives  221 us
    reduce_scatter x1, waiting for transfers between devices, shards(): lax.psum_scatter(grad_wqkv, ('wide', 'narrow'), scatter_dimension=0, tile...  160 us
    reduce_scatter x1, waiting for transfers between devices, shards(): lax.psum_scatter(grad_wout, ('wide', 'narrow'), scatter_dimension=1, tile...  139 us
    reduce_scatter x1, waiting for transfers between devices, shards(): lax.psum_scatter(grad_wdown.astype(jnp.bfloat16), 'wide', scatter_dimensi...  130 us
    reduce_scatter x1, waiting for transfers between devices, shards(): lax.psum_scatter(grad_wup.astype(jnp.bfloat16), 'wide', scatter_dimension...  129 us
    all_gather x1, waiting for transfers between devices, shards(): lax.all_gather(w_down, 'wide', axis=1, tiled=True)  110 us
    all_gather x1, waiting for transfers between devices, shards(): lax.all_gather(w_up, 'wide', axis=0, tiled=True)  101 us
    reduce_scatter x1, waiting for transfers between devices, shards(): lax.psum_scatter(grad_wgate.astype(jnp.bfloat16), 'wide', scatter_dimensi...  75.3 us
  transfers between devices with their start and end apart: 16, of which 13 were waited for; matrix products, arithmetic and copies ran while one was open for 8% of the time, Pallas kernels for 0%

profile of v1, /device:TPU:0, one launch (start us, length us, event | category | flops | bytes accessed | tf_op | source)
XLA Modules:
  0.0 1362.1 jit_solution(402545587067789494)
XLA Ops:
  12.3 7.4 all-to-all-start
  20.6 177.8 %all-reduce.11 = (bf16[2048]{0:T(1024)(128)(2,1)S(1)}, bf16[1536]{0:T(1024)(128)(2,1)S(1)}, bf16[1536]{0:T(1024)(128)(2,1)S(1)}) all-reduce(bf16[2048]{0:T(1024)(128)(2,1)S(1)} %dynamic-update-slice.1, bf16[1536]{0:T(1024)(128)(2,1)S(1)} %dynamic-update-slice, ...), channel_id=1, replica_groups=mesh['wide'=8,'narrow'=4] {'wide','narrow'}, use_global_device_ids=true, to_apply=%add.5 | all-reduce | flops 5120 | bytes 20480
  200.3 3.9 convolution_add_fusion.2
  207.2 6.5 all_gather.40
  214.6 5.9 all_gather.39
  227.4 4.2 multiply_reduce_fusion
  235.5 15.7 %all-gather.12.cloned.1.call-done = bf16[1536,2240]{1,0:T(8,128)(2,1)} async-done(((bf16[192,2240]{1,0:T(8,128)(2,1)}), bf16[1536,2240]{1,0:T(8,128)(2,1)}) %all-gather.12.cloned.1.call-update) | async-done | bytes 6881296 | tf_op jit(solution)/shard_map/all_gather | solution.py:97
  251.2 20.0 %all-gather.10.cloned.1.call-done = bf16[512,1536]{1,0:T(8,128)(2,1)} async-done(((bf16[128,1536]{1,0:T(8,128)(2,1)}), bf16[512,1536]{1,0:T(8,128)(2,1)}) %all-gather.10.cloned.1.call-update) | async-done | bytes 1572880 | tf_op jit(solution)/shard_map/all_gather | solution.py:192
  271.2 9.5 fusion.47
  280.7 100.9 %all-gather.14.cloned.1.call-done = bf16[1536,2240]{1,0:T(8,128)(2,1)} async-done(((bf16[192,2240]{1,0:T(8,128)(2,1)}), bf16[1536,2240]{1,0:T(8,128)(2,1)}) %all-gather.14.cloned.1.call-update) | async-done | bytes 6881296 | tf_op jit(solution)/shard_map/all_gather | solution.py:98
  381.6 9.3 fusion.48
  390.9 9.9 all-gather.18.cloned.1.call-done
  400.8 110.4 %all-gather.16.cloned.1.call-done = bf16[2240,1536]{0,1:T(8,128)(2,1)} async-done(((bf16[2240,192]{0,1:T(8,128)(2,1)}), bf16[2240,1536]{0,1:T(8,128)(2,1)}) %all-gather.16.cloned.1.call-update) | async-done | bytes 6881296 | tf_op jit(solution)/shard_map/all_gather | solution.py:99
  511.2 13.3 multiply_convert_fusion
  524.5 7.8 fusion.49
  532.4 5.0 fusion.3
  537.5 8.8 convolution_convert_fusion.3
  546.7 17.1 %reduce-scatter.16.cloned.1.call-done = bf16[128,1536]{1,0:T(8,128)(2,1)} async-done(((bf16[512,1536]{1,0:T(8,128)(2,1)}), bf16[128,1536]{1,0:T(8,128)(2,1)}) %reduce-scatter.16.cloned.1.call-update) | async-done | bytes 393232 | tf_op jit(solution)/shard_map/reduce_scatter | solution.py:220
  567.1 27.9 %reduce-scatter.14.cloned.1.call-done = bf16[128,1536]{1,0:T(8,128)(2,1)} async-done(((bf16[512,1536]{1,0:T(8,128)(2,1)}), bf16[128,1536]{1,0:T(8,128)(2,1)}) %reduce-scatter.14.cloned.1.call-update) | async-done | bytes 393232 | tf_op jit(solution)/shard_map/reduce_scatter | solution.py:198
  598.4 3.9 convolution_convert_fusion.4
  616.9 8.9 convolution_convert_fusion.2
  627.3 7.6 convolution_convert_fusion.1
  636.3 7.5 convolution_convert_fusion
  645.1 5.0 fusion.28
  656.6 6.4 fusion.31
  663.2 5.1 fusion.17
  668.4 43.0 %all-reduce.10 = (f32[2048]{0:T(1024)S(1)}, f32[1536]{0:T(1024)S(1)}, f32[1536]{0:T(1024)S(1)}) all-reduce(f32[2048]{0:T(1024)S(1)} %convert_reduce_fusion, f32[1536]{0:T(1024)S(1)} %get-tuple-element.83, f32[1536]{0:T(1024)S(1)} %copy-done.21), channel_id=8, replica_groups=mesh['wide'=8,'narrow'=4] {'wide','narrow'}, use_global_device_ids=true, to_apply=%region_16.17.clone | all-reduce | flops 5120 | bytes 40960
  714.3 75.3 %reduce-scatter.22.cloned.1.call-done = bf16[192,2240]{1,0:T(8,128)(2,1)} async-done(((bf16[1536,2240]{1,0:T(8,128)(2,1)}), bf16[192,2240]{1,0:T(8,128)(2,1)}) %reduce-scatter.22.cloned.1.call-update) | async-done | bytes 860176 | tf_op jit(solution)/shard_map/reduce_scatter | solution.py:314
  792.0 129.4 %reduce-scatter.24.cloned.1.call-done = bf16[192,2240]{1,0:T(8,128)(2,1)} async-done(((bf16[1536,2240]{1,0:T(8,128)(2,1)}), bf16[192,2240]{1,0:T(8,128)(2,1)}) %reduce-scatter.24.cloned.1.call-update) | async-done | bytes 860176 | tf_op jit(solution)/shard_map/reduce_scatter | solution.py:317
  923.9 129.5 %reduce-scatter.26.cloned.1.call-done = bf16[2240,192]{0,1:T(8,128)(2,1)} async-done(((bf16[2240,1536]{0,1:T(8,128)(2,1)}), bf16[2240,192]{0,1:T(8,128)(2,1)}) %reduce-scatter.26.cloned.1.call-update) | async-done | bytes 860176 | tf_op jit(solution)/shard_map/reduce_scatter | solution.py:320
  1055.9 139.2 %reduce-scatter.20.cloned.1.call-done = f32[1536,48]{0,1:T(8,128)} async-done(((f32[1536,1536]{0,1:T(8,128)}), f32[1536,48]{0,1:T(8,128)}) %reduce-scatter.20.cloned.1.call-update) | async-done | bytes 294928 | tf_op jit(solution)/shard_map/reduce_scatter | solution.py:309
  1195.1 160.3 %reduce-scatter.18.cloned.1.call-done = f32[48,2048]{1,0:T(8,128)} async-done(((f32[1536,2048]{1,0:T(8,128)}), f32[48,2048]{1,0:T(8,128)}) %reduce-scatter.18.cloned.1.call-update) | async-done | bytes 393232 | tf_op jit(solution)/shard_map/reduce_scatter | solution.py:307
  (189 shorter events, 64.8 us)
Async XLA Ops:
  7.2 193.1 %all-gather.8.cloned.1.call-start = ((), (), s32[]{:S(2)}) async-start(), calls=%async_computation.10 | async-start | bytes 6488064 | tf_op jit(solution)/shard_map/all_gather | solution.py:90
  7.9 243.3 %all-gather.12.cloned.1.call-start = ((), (), s32[]{:S(2)}) async-start(), calls=%async_computation.12 | async-start | bytes 7962624 | tf_op jit(solution)/shard_map/all_gather | solution.py:97
  12.3 7.5 copy-start.33
  12.3 7.8 copy-start.34
  12.3 8.1 copy-start.35
  12.3 186.1 %copy-start.36 = (s32[1,8]{1,0:T(1,128)S(1)}, s32[1,8]{1,0:T(1,128)}, u32[]{:S(2)}) copy-start(s32[1,8]{1,0:T(1,128)} %param.12) | copy-start | bytes 100
  12.3 187.1 %copy-start.3 = (bf16[1,128,1536]{2,1,0:T(8,128)(2,1)S(1)}, bf16[1,128,1536]{2,1,0:T(8,128)(2,1)}, u32[]{:S(2)}) copy-start(bf16[1,128,1536]{2,1,0:T(8,128)(2,1)} %param.11) | copy-start | bytes 1179652
  12.3 215.1 %all-to-all-start = ((bf16[32,1536,48]{1,2,0:T(8,128)(2,1)}), bf16[32,1536,48]{1,2,0:T(8,128)(2,1)}, u32[]{:S(2)}, u32[]{:S(2)}) async-start(bf16[32,1536,48]{1,2,0:T(8,128)(2,1)} %stack.2), calls=%async_computation | async-start | bytes 9437184 | tf_op jit(solution)/shard_map/all_to_all | solution.py:81
  19.7 251.5 %all-gather.10.cloned.1.call-start = ((), (), s32[]{:S(2)}) async-start(), calls=%async_computation.11 | async-start | bytes 1966080 | tf_op jit(solution)/shard_map/all_gather | solution.py:192
  199.1 5.6 copy-start.11
  199.1 5.6 copy-start.13
  199.2 6.0 copy-start.16
  199.2 6.0 copy-start.18
  233.5 148.1 %all-gather.14.cloned.1.call-start = ((), (), s32[]{:S(2)}) async-start(), calls=%async_computation.13 | async-start | bytes 7962624 | tf_op jit(solution)/shard_map/all_gather | solution.py:98
  234.1 166.7 %all-gather.18.cloned.1.call-start = ((), (), s32[]{:S(2)}) async-start(), calls=%async_computation.22 | async-start | bytes 1966080 | tf_op jit(solution)/shard_map/all_gather | solution.py:211
  234.7 276.5 %all-gather.16.cloned.1.call-start = ((), (), s32[]{:S(2)}) async-start(), calls=%async_computation.14 | async-start | bytes 7962624 | tf_op jit(solution)/shard_map/all_gather | solution.py:99
  235.3 328.5 %reduce-scatter.16.cloned.1.call-start = ((), (), s32[]{:S(2)}) async-start(), calls=%async_computation.16 | async-start | bytes 1966080 | tf_op jit(solution)/shard_map/reduce_scatter | solution.py:220
  524.5 7.8 copy-start.38
  524.5 7.9 copy-start.37
  524.5 7.9 copy-start.30
  537.4 57.6 %reduce-scatter.14.cloned.1.call-start = ((), (), s32[]{:S(2)}) async-start(), calls=%async_computation.15 | async-start | bytes 1966080 | tf_op jit(solution)/shard_map/reduce_scatter | solution.py:198
  546.3 105.9 %reduce-scatter.28.cloned.1.call-start = ((), (), s32[]{:S(2)}) async-start(), calls=%async_computation.23 | async-start | bytes 327680
  598.4 7.1 copy-start.25
  612.4 43.2 %reduce-scatter.30.cloned.1.call-start = ((), (), s32[]{:S(2)}) async-start(), calls=%async_computation.24 | async-start | bytes 327680
  616.9 172.6 %reduce-scatter.22.cloned.1.call-start = ((), (), s32[]{:S(2)}) async-start(), calls=%async_computation.19 | async-start | bytes 7962624 | tf_op jit(solution)/shard_map/reduce_scatter | solution.py:314
  625.9 295.5 %reduce-scatter.24.cloned.1.call-start = ((), (), s32[]{:S(2)}) async-start(), calls=%async_computation.20 | async-start | bytes 7962624 | tf_op jit(solution)/shard_map/reduce_scatter | solution.py:317
  634.9 418.5 %reduce-scatter.26.cloned.1.call-start = ((), (), s32[]{:S(2)}) async-start(), calls=%async_computation.21 | async-start | bytes 7962624 | tf_op jit(solution)/shard_map/reduce_scatter | solution.py:320
  643.9 551.2 %reduce-scatter.20.cloned.1.call-start = ((), (), s32[]{:S(2)}) async-start(), calls=%async_computation.18 | async-start | bytes 9732096 | tf_op jit(solution)/shard_map/reduce_scatter | solution.py:309
  650.1 6.4 copy-start.23
  650.1 705.2 %reduce-scatter.18.cloned.1.call-start = ((), (), s32[]{:S(2)}) async-start(), calls=%async_computation.17 | async-start | bytes 12976128 | tf_op jit(solution)/shard_map/reduce_scatter | solution.py:307
  663.2 5.1 copy-start.21
  663.2 49.9 %copy-start.28 = (f32[128]{0:T(128)S(1)}, f32[128]{0:T(128)}, u32[]{:S(2)}) copy-start(f32[128]{0:T(128)} %copy-done.27) | copy-start | bytes 1540
  (23 other events, 40.5 us)
Sparse Core Ops, SparseCore 0:
  10.8 123.2 all-gather.7
  136.4 114.8 all-gather.11
  253.4 17.7 all-gather.9
  273.3 108.2 all-gather.13
  383.0 17.7 all-gather.17
  402.9 108.2 all-gather.15
  537.6 26.2 reduce-scatter.15
  566.9 28.0 reduce-scatter.13
  612.5 20.0 reduce-scatter.27
  635.5 20.0 reduce-scatter.29
  659.3 130.2 reduce-scatter.21
  793.1 128.2 reduce-scatter.23
  925.1 128.2 reduce-scatter.25
  1059.8 135.2 reduce-scatter.19
  1201.5 153.7 reduce-scatter.17
